TPU v7x, 32 devices: a whole 2x2x4 slice. The times are simulated.
32 devices in a mesh: clus: 4 (over z), seq: 8 (over y, x, core).
Axes of the slice: x: 2, y: 2, z: 4, core: 2. Of those that a mesh axis runs over, the one named last changes fastest.
Arguments:
- embeddings: bfloat16 [8192, 768], P(('clus', 'seq')), parts along dimension 0, may hold values from -1 to 1, as said below
- doc_order: int32 [32, 256], P(('clus', 'seq')), parts along dimension 0, may hold values from 0 to 255, each once within a row
Outputs:
- prior_max: float32 [8192], P(('clus', 'seq')), parts along dimension 0
- later_max: float32 [8192], P(('clus', 'seq')), parts along dimension 0
There are 4 independent parts, one for each index of `clus`. A program takes and returns all parts, laid end to end along the dimension named above; each array names one. Nothing has to cross between parts.
Inputs may be any that keep to these rules, and one draw needn't show every extreme that they name: `embeddings`: each row has unit Euclidean length up to bfloat16 rounding. `doc_order`: each row is a permutation of 0 to 255.
All inputs are finite; a program needn't handle non-finite values.
Results may differ from a plain program's by a relative error of at most 0.0003.
Values may be sent and summed in bfloat16 or wider, within the bound.
A program may use at most 64 MiB of HBM per device.

v0:
```python
import jax
import jax.numpy as jnp
from jax import lax
from jax.sharding import PartitionSpec as P


def passed_along(block, axis, distance):
    devices = range(lax.axis_size(axis))
    route = [((i - distance) % len(devices), i) for i in devices]
    return lax.ppermute(block, axis, route)


def similar(left_rows, right_rows):
    return jnp.einsum("rd,cd->rc", left_rows, right_rows, preferred_element_type=jnp.float32)


def masked_rowmax(matrix, keep):
    return jnp.max(jnp.where(keep, matrix, jnp.float32(-1.0)), axis=1)


def per_device(embeddings, doc_order):
    ranking = doc_order[0]
    position = lax.axis_index("seq")
    members = lax.axis_size("seq")
    block_rows = embeddings.shape[0]
    self_sims = similar(embeddings, embeddings)
    prior_start = masked_rowmax(self_sims, ranking[None, :] < ranking[:, None])
    later_start = masked_rowmax(self_sims, ranking[None, :] > ranking[:, None])
    halfway = members // 2
    table_init = jnp.full((members, 2, block_rows), -1.0, jnp.float32)

    def visit(turn_index, carried):
        visitor, prior_now, later_now, table = carried
        visitor = passed_along(visitor, "seq", 1)
        sims_here = similar(embeddings, visitor)
        row_best = jnp.max(sims_here, axis=1)
        column_best = jnp.max(sims_here, axis=0)
        wrapped = turn_index > position
        active = (turn_index < halfway) | (position >= halfway)
        source = (position - turn_index + members) % members
        prior_now = jnp.where(
            active & jnp.logical_not(wrapped), jnp.maximum(prior_now, row_best), prior_now
        )
        later_now = jnp.where(active & wrapped, jnp.maximum(later_now, row_best), later_now)
        negative = jnp.full((block_rows,), -1.0, jnp.float32)
        entry_prior = jnp.where(active & wrapped, column_best, negative)
        entry_later = jnp.where(active & jnp.logical_not(wrapped), column_best, negative)
        entry = jnp.stack([entry_prior, entry_later], axis=0)[None]
        table = lax.dynamic_update_slice(table, entry, (source, jnp.int32(0), jnp.int32(0)))
        return (visitor, prior_now, later_now, table)

    visitor, prior_now, later_now, table = lax.fori_loop(
        1, halfway + 1, visit, (embeddings, prior_start, later_start, table_init)
    )
    received = lax.all_to_all(table, "seq", split_axis=0, concat_axis=0, tiled=True)
    best_seen = jnp.max(received, axis=0)
    prior_max = jnp.maximum(prior_now, best_seen[0])
    later_max = jnp.maximum(later_now, best_seen[1])
    return (prior_max, later_max)


def solution(mesh):
    return jax.shard_map(
        per_device,
        mesh=mesh,
        in_specs=(P(("clus", "seq"), None), P(("clus", "seq"), None)),
        out_specs=(P(("clus", "seq")), P(("clus", "seq"))),
        check_vma=False,
    )
```

profile of v0, /device:TPU:0, one launch (start us, length us, event | category | flops | bytes accessed | tf_op | source)
XLA Modules:
  0.0 47.2 jit_solution(2741517924942431600)
XLA Ops:
  0.6 0.0 copy-start
  0.6 1.1 %copy.6 = bf16[256,768]{1,0:T(8,128)(2,1)S(1)} copy(bf16[256,768]{1,0:T(8,128)(2,1)} %param.4) | data formatting | bytes 786432
  1.7 0.0 copy-start.1
  1.7 0.0 copy-done
  1.7 0.6 %copy-done.1 = s32[1,256]{1,0:T(1,128)S(1)} copy-done((s32[1,256]{1,0:T(1,128)S(1)}, s32[1,256]{1,0:T(1,128)}, u32[]{:S(2)}) %copy-start.1) | copy-done | bytes 1048
  2.4 0.3 select_reduce_fusion
  2.8 35.2 %while.21 = (s32[]{:T(128)}, bf16[256,768]{1,0:T(8,128)(2,1)S(1)}, f32[256]{0:T(256)S(1)}, f32[256]{0:T(256)S(1)}, f32[8,2,256]{2,1,0:T(2,128)S(1)}, /*index=5*/...) while((s32[]{:T(128)}, bf16[256,768]{1,0:T(8,128)(2,1)S(1)}, ...), condition=%wide.region_5.6_spmd, body=%wide.region_2.5_spmd.sunk | while | flops 100795904 | bytes 3160431 | solution.py:52
  2.8 0.5 %collective-permute-start = (bf16[256,768]{1,0:T(8,128)(2,1)S(1)}, bf16[256,768]{1,0:T(8,128)(2,1)S(1)}, u32[]{:S(2)}, u32[]{:S(2)}) collective-permute-start(bf16[256,768]{1,0:T(8,128)(2,1)S(1)} %get-tuple-element.293), channel_id=1, source_target_pairs={{7,0},{0,1},{1,2},{2,3},{3,4},{4,5},{5,6},{6,7},{15,8},{8,9},{9,10... | collective-permute-start | bytes 1179656 | tf_op jit(solution)/shard_map/while/body/eval_jaxpr/ppermute | solution.py:10
  3.3 8.3 %collective-permute-done = bf16[256,768]{1,0:T(8,128)(2,1)S(1)} collective-permute-done((bf16[256,768]{1,0:T(8,128)(2,1)S(1)}, bf16[256,768]{1,0:T(8,128)(2,1)S(1)}, u32[]{:S(2)}, u32[]{:S(2)}) %collective-permute-start) | collective-permute-done | bytes 393248 | tf_op jit(solution)/shard_map/while/body/eval_jaxpr/ppermute | solution.py:10
  11.6 0.4 fusion.13
  12.1 0.1 collective-permute-start
  12.2 8.0 %collective-permute-done = bf16[256,768]{1,0:T(8,128)(2,1)S(1)} collective-permute-done((bf16[256,768]{1,0:T(8,128)(2,1)S(1)}, bf16[256,768]{1,0:T(8,128)(2,1)S(1)}, u32[]{:S(2)}, u32[]{:S(2)}) %collective-permute-start) | collective-permute-done | bytes 393248 | tf_op jit(solution)/shard_map/while/body/eval_jaxpr/ppermute | solution.py:10
  20.3 0.4 fusion.13
  20.7 0.1 collective-permute-start
  20.8 8.0 %collective-permute-done = bf16[256,768]{1,0:T(8,128)(2,1)S(1)} collective-permute-done((bf16[256,768]{1,0:T(8,128)(2,1)S(1)}, bf16[256,768]{1,0:T(8,128)(2,1)S(1)}, u32[]{:S(2)}, u32[]{:S(2)}) %collective-permute-start) | collective-permute-done | bytes 393248 | tf_op jit(solution)/shard_map/while/body/eval_jaxpr/ppermute | solution.py:10
  28.9 0.4 fusion.13
  29.4 0.1 collective-permute-start
  29.5 8.0 %collective-permute-done = bf16[256,768]{1,0:T(8,128)(2,1)S(1)} collective-permute-done((bf16[256,768]{1,0:T(8,128)(2,1)S(1)}, bf16[256,768]{1,0:T(8,128)(2,1)S(1)}, u32[]{:S(2)}, u32[]{:S(2)}) %collective-permute-start) | collective-permute-done | bytes 393248 | tf_op jit(solution)/shard_map/while/body/eval_jaxpr/ppermute | solution.py:10
  37.5 0.4 fusion.13
  38.0 8.1 %all_to_all.5 = f32[8,2,256]{2,1,0:T(2,128)S(1)} all-to-all(f32[8,2,256]{2,1,0:T(2,128)S(1)} %get-tuple-element.188), channel_id=1, replica_groups=mesh['clus'=4,'seq'=8] {'seq'}, dimensions={0} | all-to-all | bytes 32768 | tf_op jit(solution)/shard_map/all_to_all | solution.py:55
  46.1 0.6 %max.27 = f32[256]{0:T(256)} maximum(f32[256]{0:T(256)S(1)} %get-tuple-element.189, f32[256]{0:T(256)S(1)} %bitcast.26) | non-fusion elementwise | flops 256 | bytes 3072 | tf_op jit(solution)/shard_map/max | solution.py:58
  46.7 0.6 %max.26 = f32[256]{0:T(256)} maximum(f32[256]{0:T(256)S(1)} %get-tuple-element.187, f32[256]{0:T(256)S(1)} %bitcast.25) | non-fusion elementwise | flops 256 | bytes 3072 | tf_op jit(solution)/shard_map/max | solution.py:57
  (15 shorter events, 0.3 us)
Async XLA Ops:
  0.6 1.1 %copy-start = (bf16[256,768]{1,0:T(8,128)(2,1)S(1)}, bf16[256,768]{1,0:T(8,128)(2,1)}, u32[]{:S(2)}) copy-start(bf16[256,768]{1,0:T(8,128)(2,1)} %param.4) | copy-start | bytes 1179652
  1.7 0.7 %copy-start.1 = (s32[1,256]{1,0:T(1,128)S(1)}, s32[1,256]{1,0:T(1,128)}, u32[]{:S(2)}) copy-start(s32[1,256]{1,0:T(1,128)} %param.5) | copy-start | bytes 3076
  2.8 8.9 %collective-permute-start = (bf16[256,768]{1,0:T(8,128)(2,1)S(1)}, bf16[256,768]{1,0:T(8,128)(2,1)S(1)}, u32[]{:S(2)}, u32[]{:S(2)}) collective-permute-start(bf16[256,768]{1,0:T(8,128)(2,1)S(1)} %get-tuple-element.293), channel_id=1, source_target_pairs={{7,0},{0,1},{1,2},{2,3},{3,4},{4,5},{5,6},{6,7},{15,8},{8,9},{9,10... | collective-permute-start | bytes 1179656 | tf_op jit(solution)/shard_map/while/body/eval_jaxpr/ppermute | solution.py:10
  12.1 8.2 %collective-permute-start = (bf16[256,768]{1,0:T(8,128)(2,1)S(1)}, bf16[256,768]{1,0:T(8,128)(2,1)S(1)}, u32[]{:S(2)}, u32[]{:S(2)}) collective-permute-start(bf16[256,768]{1,0:T(8,128)(2,1)S(1)} %get-tuple-element.293), channel_id=1, source_target_pairs={{7,0},{0,1},{1,2},{2,3},{3,4},{4,5},{5,6},{6,7},{15,8},{8,9},{9,10... | collective-permute-start | bytes 1179656 | tf_op jit(solution)/shard_map/while/body/eval_jaxpr/ppermute | solution.py:10
  20.7 8.2 %collective-permute-start = (bf16[256,768]{1,0:T(8,128)(2,1)S(1)}, bf16[256,768]{1,0:T(8,128)(2,1)S(1)}, u32[]{:S(2)}, u32[]{:S(2)}) collective-permute-start(bf16[256,768]{1,0:T(8,128)(2,1)S(1)} %get-tuple-element.293), channel_id=1, source_target_pairs={{7,0},{0,1},{1,2},{2,3},{3,4},{4,5},{5,6},{6,7},{15,8},{8,9},{9,10... | collective-permute-start | bytes 1179656 | tf_op jit(solution)/shard_map/while/body/eval_jaxpr/ppermute | solution.py:10
  29.4 8.2 %collective-permute-start = (bf16[256,768]{1,0:T(8,128)(2,1)S(1)}, bf16[256,768]{1,0:T(8,128)(2,1)S(1)}, u32[]{:S(2)}, u32[]{:S(2)}) collective-permute-start(bf16[256,768]{1,0:T(8,128)(2,1)S(1)} %get-tuple-element.293), channel_id=1, source_target_pairs={{7,0},{0,1},{1,2},{2,3},{3,4},{4,5},{5,6},{6,7},{15,8},{8,9},{9,10... | collective-permute-start | bytes 1179656 | tf_op jit(solution)/shard_map/while/body/eval_jaxpr/ppermute | solution.py:10
where the time goes:
time: 47.4 us; the launch traced here: 47.2 us
  waiting for transfers between devices  32.5 us (69%)
  blocking collectives  8.1 us (17%)
  local copies, waits for them, and re-layouts  1.87 us (4%)
  matrix products  1.85 us (4%)
  other arithmetic  1.3 us (3%)
  starting transfers between devices  0.72 us (2%)
  between operations  0.67 us (1%)
    ppermute x4, waiting for transfers between devices, passed_along(): return lax.ppermute(block, axis, route)  32.5 us
    all_to_all x1, blocking collectives, per_device(): lax.all_to_all(table, 'seq', split_axis=0, concat_axis=0, tiled=True)  8.1 us
    dot_general x5, matrix products, similar(): jnp.einsum('rd,cd->rc', left_rows, right_rows, preferred_element_type=jnp...  1.85 us
    unnamed x5, local copies, waits for them, and re-layouts  1.75 us
  transfers between devices with their start and end apart: 4, of which 4 were waited for; matrix products, arithmetic and copies ran while one was open for 0% of the time, Pallas kernels for 0%

commit v1 on v0

--- a/solution.py
+++ b/solution.py
@@ -1,7 +1,145 @@
+import functools
+
 import jax
 import jax.numpy as jnp
 from jax import lax
+from jax.experimental import pallas as pl
+from jax.experimental.pallas import tpu as pltpu
 from jax.sharding import PartitionSpec as P
+
+MESH = pl.DeviceIdType.MESH
+PIECES = 2
+
+
+def column_max(left, right):
+    sims = lax.dot_general(
+        left, right, (((1,), (1,)), ((), ())), preferred_element_type=jnp.float32
+    )
+    return jnp.max(sims, axis=0, keepdims=True)
+
+
+def exchange_kernel(
+    emb_hbm, rank_ref, prior_ref, later_ref,
+    own, mate, xblk, yblk, mate_out, x_out, y_out, mate_in, x_in, y_in,
+    load_sem, mate_sems, x_send, x_recv, y_send, y_recv, back_send, back_recv,
+):
+    me = lax.axis_index("seq")
+    core, xbit, ybit = me % 2, (me // 2) % 2, me // 4
+    rows = own.shape[0]
+    piece = rows // PIECES
+    mate_id = me + 1 - 2 * core
+    x_id = me + 2 - 4 * xbit + ybit * (1 - 2 * core)
+    y_id = me + 4 - 8 * ybit
+
+    load = pltpu.make_async_copy(emb_hbm, own, load_sem)
+    load.start()
+    barrier = pltpu.get_barrier_semaphore()
+    for other in (mate_id, x_id, y_id):
+        pl.semaphore_signal(barrier, inc=1, device_id={"seq": other}, device_id_type=MESH)
+    load.wait()
+    pl.semaphore_wait(barrier, 3)
+
+    def send(src, dst, send_sem, recv_sem, other):
+        copy = pltpu.make_async_remote_copy(
+            src_ref=src, dst_ref=dst, send_sem=send_sem, recv_sem=recv_sem,
+            device_id={"seq": other}, device_id_type=MESH,
+        )
+        copy.start()
+        return copy
+
+    x_copies, y_copies = [], []
+    for k in range(PIECES):
+        part = pl.ds(k * piece, piece)
+        x_copies.append(send(own.at[part], xblk.at[part], x_send.at[k], x_recv.at[k], x_id))
+        y_copies.append(send(own.at[part], yblk.at[part], y_send.at[k], y_recv.at[k], y_id))
+    mate_copy = send(own, mate, mate_sems.at[0], mate_sems.at[1], mate_id)
+
+    lowest = jnp.full((1, rows), -1.0, jnp.float32)
+    across = jnp.broadcast_to(rank_ref[...].astype(jnp.float32), (rows, rows))
+    down = across.T
+    self_sims = lax.dot_general(
+        own[...], own[...], (((1,), (1,)), ((), ())), preferred_element_type=jnp.float32
+    )
+    prior = jnp.max(jnp.where(down < across, self_sims, -1.0), axis=0, keepdims=True)
+    later = jnp.max(jnp.where(down > across, self_sims, -1.0), axis=0, keepdims=True)
+
+    def fold(prior, later, values, is_prior):
+        return (
+            jnp.maximum(prior, jnp.where(is_prior, values, lowest)),
+            jnp.maximum(later, jnp.where(is_prior, lowest, values)),
+        )
+
+    mate_copy.wait_recv()
+    prior, later = fold(prior, later, column_max(mate[...], own[...]), core == 1)
+
+    own_x = own_y = mate_x = mate_y = lowest
+    x_best = [lowest[:, :piece]] * PIECES
+    y_best = [lowest[:, :piece]] * PIECES
+
+    def meet(best, count, left, right):
+        found = column_max(left, right)
+        return [
+            jnp.maximum(b, found[:, j * piece:(j + 1) * piece]) if j < count else b
+            for j, b in enumerate(best)
+        ]
+
+    for k in range(PIECES):
+        x_copies[k].wait_recv()
+        y_copies[k].wait_recv()
+        start, end = k * piece, (k + 1) * piece
+        y_best = meet(y_best, k + 1, xblk[start:end], yblk[:end])
+        x_best = meet(x_best, k + 1, yblk[start:end], xblk[:end])
+        if k:
+            y_best[k] = jnp.maximum(y_best[k], column_max(xblk[:start], yblk[start:end]))
+            x_best[k] = jnp.maximum(x_best[k], column_max(yblk[:start], xblk[start:end]))
+        if k == PIECES - 1:
+            x_out[...] = jnp.concatenate(x_best, axis=1)
+            y_out[...] = jnp.concatenate(y_best, axis=1)
+            x_back = send(x_out, x_in, back_send.at[0], back_recv.at[0], x_id)
+            y_back = send(y_out, y_in, back_send.at[1], back_recv.at[1], y_id)
+        mate_x = jnp.maximum(mate_x, column_max(xblk[start:end], mate[...]))
+        mate_y = jnp.maximum(mate_y, column_max(yblk[start:end], mate[...]))
+        if k == PIECES - 1:
+            mate_out[0:1, :] = mate_x
+            mate_out[1:2, :] = mate_y
+            mate_back = send(mate_out, mate_in, back_send.at[2], back_recv.at[2], mate_id)
+        own_x = jnp.maximum(own_x, column_max(xblk[start:end], own[...]))
+        own_y = jnp.maximum(own_y, column_max(yblk[start:end], own[...]))
+
+    mate_back.wait_recv()
+    chip, x_chip, y_chip = 2 * ybit + xbit, 2 * ybit + 1 - xbit, 2 - 2 * ybit + xbit
+    far_chip = 3 - chip
+    prior, later = fold(prior, later, jnp.maximum(own_x, mate_in[0:1, :]), x_chip < chip)
+    prior, later = fold(prior, later, jnp.maximum(own_y, mate_in[1:2, :]), y_chip < chip)
+    x_back.wait_recv()
+    y_back.wait_recv()
+    prior, later = fold(prior, later, jnp.maximum(x_in[...], y_in[...]), far_chip < chip)
+    prior_ref[...] = prior
+    later_ref[...] = later
+    for copy in [*x_copies, *y_copies, mate_copy, x_back, y_back, mate_back]:
+        copy.wait_send()
+
+
+def exchange(embeddings, doc_order):
+    rows, width = embeddings.shape
+    block = pltpu.VMEM((rows, width), embeddings.dtype)
+    one, two = pltpu.VMEM((1, rows), jnp.float32), pltpu.VMEM((2, rows), jnp.float32)
+    dma = pltpu.SemaphoreType.DMA
+    result = jax.ShapeDtypeStruct((1, rows), jnp.float32)
+    vmem = pl.BlockSpec(memory_space=pltpu.VMEM)
+    prior, later = pl.pallas_call(
+        exchange_kernel,
+        out_shape=(result, result),
+        in_specs=[pl.BlockSpec(memory_space=pl.ANY), vmem],
+        out_specs=(vmem, vmem),
+        scratch_shapes=[
+            block, block, block, block, two, one, one, two, one, one,
+            dma, dma((2,)), dma((PIECES,)), dma((PIECES,)), dma((PIECES,)), dma((PIECES,)),
+            dma((3,)), dma((3,)),
+        ],
+        compiler_params=pltpu.CompilerParams(collective_id=0, has_side_effects=True),
+    )(embeddings, doc_order)
+    return prior.reshape(rows), later.reshape(rows)
 
 
 def passed_along(block, axis, distance):
@@ -18,7 +156,7 @@
     return jnp.max(jnp.where(keep, matrix, jnp.float32(-1.0)), axis=1)
 
 
-def per_device(embeddings, doc_order):
+def ring_exchange(embeddings, doc_order):
     ranking = doc_order[0]
     position = lax.axis_index("seq")
     members = lax.axis_size("seq")
@@ -59,6 +197,12 @@
     return (prior_max, later_max)
 
 
+def per_device(embeddings, doc_order):
+    if lax.axis_size("seq") == 2 ** 3:
+        return exchange(embeddings, doc_order)
+    return ring_exchange(embeddings, doc_order)
+
+
 def solution(mesh):
     return jax.shard_map(
         per_device,

time: 47.4 us -> 20.8 us (0.44)
  waiting for transfers between devices: 32.5 us -> 0 us
  Pallas kernels: 0 us -> 18.1 us
  blocking collectives: 8.1 us -> 0 us
  matrix products: 1.85 us -> 0 us
  other arithmetic: 1.3 us -> 0 us
  starting transfers between devices: 0.72 us -> 0 us
    ppermute x4 -> x0, waiting for transfers between devices: 32.5 us -> none  [passed_along(): return lax.ppermute(block, axis, route)]
    pallas_call x0 -> x1, Pallas kernels: none -> 18.1 us  [exchange(): pl.pallas_call(exchange_kernel, out_shape=(result, result), in_specs=[pl....]
    all_to_all x1 -> x0, blocking collectives: 8.1 us -> none  [per_device(): lax.all_to_all(table, 'seq', split_axis=0, concat_axis=0, tiled=True)]
    dot_general x5 -> x0, matrix products: 1.85 us -> none  [similar(): jnp.einsum('rd,cd->rc', left_rows, right_rows, preferred_element_type=jnp...]
    max x2 -> x0, other arithmetic: 1.13 us -> none  [the longest x1 0.57 us: per_device(): later_max = jnp.maximum(later_now, best_seen[1])]
    ppermute x4 -> x0, starting transfers between devices: 0.72 us -> none  [passed_along(): return lax.ppermute(block, axis, route)]
    unnamed x5 -> x6, local copies, waits for them, and re-layouts: 1.75 us -> 1.86 us
  transfers between devices with their start and end apart: 4 -> 0, of which waited for: 4 -> 0; matrix products, arithmetic and copies ran while one was open for 0% -> 0% of each run, Pallas kernels for 0% -> 0%
where the time goes in v1:
time: 20.8 us; the launch traced here: 20.6 us
  Pallas kernels  18.1 us (87%)
  local copies, waits for them, and re-layouts  1.86 us (9%)
  between operations  0.65 us (3%)
    pallas_call x1, Pallas kernels, exchange(): pl.pallas_call(exchange_kernel, out_shape=(result, result), in_specs=[pl....  18.1 us
    unnamed x6, local copies, waits for them, and re-layouts  1.86 us

profile of v1, /device:TPU:0, one launch (start us, length us, event | category | flops | bytes accessed | tf_op | source)
XLA Modules:
  0.0 20.6 jit_solution(5122977035396529694)
XLA Ops:
  0.6 18.1 %shard_map.41 = (f32[1,256]{1,0:T(1,128)}, f32[1,256]{1,0:T(1,128)}) custom-call(bf16[256,768]{1,0:T(8,128)(2,1)} %emb_hbm.1, s32[1,256]{1,0:T(1,128)} %rank_ref.1), custom_call_target="tpu_custom_call" | custom-call | tf_op jit(solution)/shard_map/pallas_call | solution.py:130
  18.7 0.0 copy-start.1
  18.7 0.7 %copy-done.1 = f32[1,256]{1,0:T(1,128)S(1)} copy-done((f32[1,256]{1,0:T(1,128)S(1)}, f32[1,256]{1,0:T(1,128)}, u32[]{:S(2)}) %copy-start.1) | copy-done | bytes 1048
  19.4 0.0 copy-start
  19.4 0.6 %copy.6 = f32[256]{0:T(256)} copy(f32[256]{0:T(256)S(1)} %bitcast.3) | data formatting | bytes 2048
  19.9 0.1 copy-done
  20.0 0.6 %copy.7 = f32[256]{0:T(256)} copy(f32[256]{0:T(256)S(1)} %bitcast.2) | data formatting | bytes 2048
Async XLA Ops:
  18.7 0.7 %copy-start.1 = (f32[1,256]{1,0:T(1,128)S(1)}, f32[1,256]{1,0:T(1,128)}, u32[]{:S(2)}) copy-start(f32[1,256]{1,0:T(1,128)} %get-tuple-element.4) | copy-start | bytes 3076
  19.4 0.6 %copy-start = (f32[1,256]{1,0:T(1,128)S(1)}, f32[1,256]{1,0:T(1,128)}, u32[]{:S(2)}) copy-start(f32[1,256]{1,0:T(1,128)} %get-tuple-element.5) | copy-start | bytes 3076

commit v2 on v1

--- a/solution.py
+++ b/solution.py
@@ -19,9 +19,9 @@
 
 
 def exchange_kernel(
-    emb_hbm, rank_ref, prior_ref, later_ref,
-    own, mate, xblk, yblk, mate_out, x_out, y_out, mate_in, x_in, y_in,
-    load_sem, mate_sems, x_send, x_recv, y_send, y_recv, back_send, back_recv,
+    emb_hbm, rank_hbm, result_ref,
+    rank, own, mate, xblk, yblk, mate_out, x_out, y_out, mate_in, x_in, y_in,
+    load_sem, rank_sem, mate_sems, x_send, x_recv, y_send, y_recv, back_send, back_recv,
 ):
     me = lax.axis_index("seq")
     core, xbit, ybit = me % 2, (me // 2) % 2, me // 4
@@ -33,6 +33,8 @@
 
     load = pltpu.make_async_copy(emb_hbm, own, load_sem)
     load.start()
+    rank_load = pltpu.make_async_copy(rank_hbm, rank, rank_sem)
+    rank_load.start()
     barrier = pltpu.get_barrier_semaphore()
     for other in (mate_id, x_id, y_id):
         pl.semaphore_signal(barrier, inc=1, device_id={"seq": other}, device_id_type=MESH)
@@ -55,7 +57,8 @@
     mate_copy = send(own, mate, mate_sems.at[0], mate_sems.at[1], mate_id)
 
     lowest = jnp.full((1, rows), -1.0, jnp.float32)
-    across = jnp.broadcast_to(rank_ref[...].astype(jnp.float32), (rows, rows))
+    rank_load.wait()
+    across = jnp.broadcast_to(rank[...].astype(jnp.float32), (rows, rows))
     down = across.T
     self_sims = lax.dot_general(
         own[...], own[...], (((1,), (1,)), ((), ())), preferred_element_type=jnp.float32
@@ -114,8 +117,8 @@
     x_back.wait_recv()
     y_back.wait_recv()
     prior, later = fold(prior, later, jnp.maximum(x_in[...], y_in[...]), far_chip < chip)
-    prior_ref[...] = prior
-    later_ref[...] = later
+    result_ref[0:1, :] = prior
+    result_ref[1:2, :] = later
     for copy in [*x_copies, *y_copies, mate_copy, x_back, y_back, mate_back]:
         copy.wait_send()
 
@@ -125,21 +128,19 @@
     block = pltpu.VMEM((rows, width), embeddings.dtype)
     one, two = pltpu.VMEM((1, rows), jnp.float32), pltpu.VMEM((2, rows), jnp.float32)
     dma = pltpu.SemaphoreType.DMA
-    result = jax.ShapeDtypeStruct((1, rows), jnp.float32)
-    vmem = pl.BlockSpec(memory_space=pltpu.VMEM)
-    prior, later = pl.pallas_call(
+    result = pl.pallas_call(
         exchange_kernel,
-        out_shape=(result, result),
-        in_specs=[pl.BlockSpec(memory_space=pl.ANY), vmem],
-        out_specs=(vmem, vmem),
+        out_shape=two,
+        in_specs=[pl.BlockSpec(memory_space=pl.ANY)] * 2,
+        out_specs=pl.BlockSpec(memory_space=pltpu.VMEM),
         scratch_shapes=[
-            block, block, block, block, two, one, one, two, one, one,
-            dma, dma((2,)), dma((PIECES,)), dma((PIECES,)), dma((PIECES,)), dma((PIECES,)),
+            pltpu.VMEM((1, rows), doc_order.dtype), block, block, block, block, two, one, one, two, one, one,
+            dma, dma, dma((2,)), dma((PIECES,)), dma((PIECES,)), dma((PIECES,)), dma((PIECES,)),
             dma((3,)), dma((3,)),
         ],
         compiler_params=pltpu.CompilerParams(collective_id=0, has_side_effects=True),
     )(embeddings, doc_order)
-    return prior.reshape(rows), later.reshape(rows)
+    return result[0], result[1]
 
 
 def passed_along(block, axis, distance):

time: 20.8 us -> 18.2 us (0.87)
  Pallas kernels: 18.1 us -> 16.8 us
  local copies, waits for them, and re-layouts: 1.86 us -> 0.57 us
    unnamed x6 -> x0, local copies, waits for them, and re-layouts: 1.86 us -> none
    pallas_call x1, Pallas kernels: 18.1 us -> 16.8 us  [exchange(): pl.pallas_call(exchange_kernel, out_shape=two, in_specs=[pl.BlockSpec(mem...]
    slice x0 -> x1, local copies, waits for them, and re-layouts: none -> 0.57 us  [exchange(): return (result[0], result[1])]
where the time goes in v2:
time: 18.2 us; the launch traced here: 18 us
  Pallas kernels  16.8 us (92%)
  between operations  0.64 us (4%)
  local copies, waits for them, and re-layouts  0.57 us (3%)
    pallas_call x1, Pallas kernels, exchange(): pl.pallas_call(exchange_kernel, out_shape=two, in_specs=[pl.BlockSpec(mem...  16.8 us
    slice x1, local copies, waits for them, and re-layouts, exchange(): return (result[0], result[1])  0.57 us

profile of v2, /device:TPU:0, one launch (start us, length us, event | category | flops | bytes accessed | tf_op | source)
XLA Modules:
  0.0 18.0 jit_solution(17143870134916354157)
XLA Ops:
  0.6 16.8 %shard_map.41 = f32[2,256]{1,0:T(2,128)S(1)} custom-call(bf16[256,768]{1,0:T(8,128)(2,1)} %emb_hbm.1, s32[1,256]{1,0:T(1,128)} %rank_hbm.1), custom_call_target="tpu_custom_call" | custom-call | tf_op jit(solution)/shard_map/pallas_call | solution.py:131
  17.5 0.6 %fusion = (f32[1,256]{1,0:T(1,128)}, f32[1,256]{1,0:T(1,128)}) fusion(f32[2,256]{1,0:T(2,128)S(1)} %shard_map.41), kind=kLoop, calls=%fused_computation | loop fusion | bytes 4096 | tf_op jit(solution)/shard_map/slice | solution.py:143

commit v3 on v2

--- a/solution.py
+++ b/solution.py
@@ -8,7 +8,7 @@
 from jax.sharding import PartitionSpec as P
 
 MESH = pl.DeviceIdType.MESH
-PIECES = 2
+PIECES = 1
 
 
 def column_max(left, right):
@@ -28,16 +28,16 @@
     rows = own.shape[0]
     piece = rows // PIECES
     mate_id = me + 1 - 2 * core
-    x_id = me + 2 - 4 * xbit + ybit * (1 - 2 * core)
-    y_id = me + 4 - 8 * ybit
-
+    x_id = me + 2 - 4 * xbit + (1 - 2 * core)
+    y_id = me + 4 - 8 * ybit + (1 - xbit) * (1 - 2 * core)
+
+    barrier = pltpu.get_barrier_semaphore()
+    for other in (x_id, y_id, mate_id):
+        pl.semaphore_signal(barrier, inc=1, device_id={"seq": other}, device_id_type=MESH)
     load = pltpu.make_async_copy(emb_hbm, own, load_sem)
     load.start()
     rank_load = pltpu.make_async_copy(rank_hbm, rank, rank_sem)
     rank_load.start()
-    barrier = pltpu.get_barrier_semaphore()
-    for other in (mate_id, x_id, y_id):
-        pl.semaphore_signal(barrier, inc=1, device_id={"seq": other}, device_id_type=MESH)
     load.wait()
     pl.semaphore_wait(barrier, 3)
 

time: 18.2 us -> 17.4 us (0.956)
  Pallas kernels: 16.8 us -> 16 us
    pallas_call x1, Pallas kernels: 16.8 us -> 16 us  [exchange(): pl.pallas_call(exchange_kernel, out_shape=two, in_specs=[pl.BlockSpec(mem...]
where the time goes in v3:
time: 17.4 us; the launch traced here: 17.2 us
  Pallas kernels  16 us (92%)
  between operations  0.64 us (4%)
  local copies, waits for them, and re-layouts  0.57 us (3%)
    pallas_call x1, Pallas kernels, exchange(): pl.pallas_call(exchange_kernel, out_shape=two, in_specs=[pl.BlockSpec(mem...  16 us
    slice x1, local copies, waits for them, and re-layouts, exchange(): return (result[0], result[1])  0.57 us

profile of v3, /device:TPU:0, one launch (start us, length us, event | category | flops | bytes accessed | tf_op | source)
XLA Modules:
  0.0 17.2 jit_solution(2008710898235555019)
XLA Ops:
  0.6 16.0 %shard_map.41 = f32[2,256]{1,0:T(2,128)S(1)} custom-call(bf16[256,768]{1,0:T(8,128)(2,1)} %emb_hbm.1, s32[1,256]{1,0:T(1,128)} %rank_hbm.1), custom_call_target="tpu_custom_call" | custom-call | tf_op jit(solution)/shard_map/pallas_call | solution.py:131
  16.6 0.6 %fusion = (f32[1,256]{1,0:T(1,128)}, f32[1,256]{1,0:T(1,128)}) fusion(f32[2,256]{1,0:T(2,128)S(1)} %shard_map.41), kind=kLoop, calls=%fused_computation | loop fusion | bytes 4096 | tf_op jit(solution)/shard_map/slice | solution.py:143
